TPU v7x, 256 devices: a 8x8x2 block of a 8x8x16 slice. The times are simulated.
256 devices in a mesh: grp: 2 (over z), row: 64 (over y, x), col: 2 (over core).
Axes of the slice: x: 8, y: 8, z: 2, core: 2. Of those that a mesh axis runs over, the one named last changes fastest.
The devices are a block of a 8x8x16 slice.
Arguments:
- factors: bfloat16 [2, 12288, 6144], P(None, ('grp', 'row'), 'col'), parts along dimension 1, may hold values from -6 to 6
- orbitals: bfloat16 [12288, 1024], P(('grp', 'row'), 'col'), parts along dimension 0, may hold values from -0.02734375 to 0.02734375
- field_term: bfloat16 [12288, 6144], P(('grp', 'row'), 'col'), parts along dimension 0, may hold values from -1.5 to 1.5
Outputs:
- fock_matrix: bfloat16 [12288, 6144], P(('grp', 'row'), 'col'), parts along dimension 0
There are 2 independent parts, one for each index of `grp`. A program takes and returns all parts, laid end to end along the dimension named above; each array names one. Nothing has to cross between parts.
All inputs are finite; a program needn't handle non-finite values.
Results may differ from a plain program's by a relative error of at most 0.02.
Values may be sent and summed in bfloat16 or wider, within the bound.
A program may use at most 64 MiB of HBM per device.

v0:
```python
import functools
import jax
import jax.numpy as jnp
from jax import lax
from jax.sharding import Mesh
from jax.sharding import PartitionSpec as P

ROW = ("row_0", "row_1")
ROW_COL = ("row_0", "row_1", "col")
GRP_ROW = ("grp", "row_0", "row_1")


def copy_for_each(value, axis):
    size = lax.axis_size(axis)
    return lax.all_to_all(
        jnp.broadcast_to(value[None], (size, *value.shape)), axis, 0, 0, tiled=True
    )


def joined_along(tiles, dim):
    tiles = jnp.moveaxis(tiles, 0, dim)
    dims = tiles.shape
    return tiles.reshape(*dims[:dim], dims[dim] * dims[dim + 1], *dims[dim + 2 :])


def collect(value, axis, dim):
    tiles = copy_for_each(value, axis)
    return joined_along(tiles, dim)


def split_up(value, dim, size):
    before, after = (value.shape[:dim], value.shape[dim + 1 :])
    return jnp.moveaxis(value.reshape(*before, size, -1, *after), dim, 0)


def sum_at_owner(value, axis, dim):
    tiles = split_up(value, dim, lax.axis_size(axis))
    arrived = lax.all_to_all(tiles, axis, split_axis=0, concat_axis=0, tiled=True)
    return arrived.astype(jnp.float32).sum(axis=0)


def by_axis(value, axes):
    return functools.reduce(lax.psum, axes, value)


def shards(factors, orbitals, field_term):
    aux_count = factors.shape[0]
    all_orbitals = lax.all_gather(orbitals, ROW, axis=0, tiled=True)
    orbit_wide = orbitals.astype(jnp.float32)
    exchange = None
    gammas = []
    for aux in range(aux_count):
        half_local = jnp.dot(
            collect(factors[aux], "col", 1), all_orbitals, preferred_element_type=jnp.float32
        ).astype(jnp.bfloat16)
        local_fit = jnp.sum(half_local.astype(jnp.float32) * orbit_wide)
        gammas.append(local_fit)
        term = lax.dot_general(
            half_local,
            lax.all_gather(half_local, ROW, axis=0, tiled=True),
            (((1,), (1,)), ((), ())),
            preferred_element_type=jnp.float32,
        )
        reduced = sum_at_owner(term.astype(jnp.bfloat16), "col", 1)
        exchange = reduced if exchange is None else exchange + reduced
    fitted = by_axis(jnp.stack(gammas), ROW_COL)
    gammas = [fitted[aux] for aux in range(aux_count)]
    coulomb = jnp.zeros(field_term.shape, jnp.float32)
    for aux in range(aux_count):
        coulomb = coulomb + gammas[aux] * factors[aux].astype(jnp.float32)
    fock_matrix = field_term.astype(jnp.float32) + coulomb - 0.25 * exchange
    return fock_matrix.astype(jnp.bfloat16)


def solution(mesh):
    finer = Mesh(
        mesh.devices.reshape(mesh.shape["grp"], 8, 8, mesh.shape["col"]),
        ("grp", "row_0", "row_1", "col"),
    )
    return jax.shard_map(
        shards,
        mesh=finer,
        in_specs=(P(None, GRP_ROW, "col"), P(GRP_ROW, "col"), P(GRP_ROW, "col")),
        out_specs=P(GRP_ROW, "col"),
        check_vma=False,
    )
```

profile of v0, /device:TPU:513, one launch (start us, length us, event | category | flops | bytes accessed | tf_op | source)
XLA Modules:
  0.0 318.9 jit_solution(6659823777059124831)
XLA Ops:
  6.5 0.0 all-gather.4.cloned.1.call-start
  6.6 0.7 all-gather.4.cloned.1.call-update
  7.3 1.3 slice_bitcast_fusion
  8.6 0.1 broadcast_in_dim.17
  8.8 24.7 %all_to_all.20 = bf16[2,96,3072]{2,1,0:T(8,128)(2,1)S(1)} all-to-all(bf16[2,96,3072]{2,1,0:T(8,128)(2,1)S(1)} %broadcast_in_dim.17), channel_id=1, replica_groups=mesh['grp'=2,'row_0'=8,'row_1'=8,'col'=2] {'col'}, dimensions={0} | all-to-all | bytes 2359296 | tf_op jit(solution)/shard_map/all_to_all | solution.py:15
  33.5 1.2 broadcast_in_dim.15
  34.7 4.0 %all-to-all-start = ((bf16[2,96,3072]{2,1,0:T(8,128)(2,1)}), bf16[2,96,3072]{2,1,0:T(8,128)(2,1)S(1)}, u32[]{:S(2)}, u32[]{:S(2)}) async-start(bf16[2,96,3072]{2,1,0:T(8,128)(2,1)} %broadcast_in_dim.15), calls=%async_computation | async-start | bytes 2359296 | tf_op jit(solution)/shard_map/all_to_all | solution.py:15
  38.7 0.0 all-gather.6.cloned.1.call-start
  38.7 0.1 copy.11
  38.8 1.7 all-to-all-done
  40.5 0.1 copy.10
  40.6 73.8 %all-gather.4.cloned.1.call-done = bf16[6144,512]{1,0:T(8,128)(2,1)} async-done(((bf16[96,512]{1,0:T(8,128)(2,1)}), bf16[6144,512]{1,0:T(8,128)(2,1)}) %all-gather.4.cloned.1.call-update) | async-done | bytes 6291472 | tf_op jit(solution)/shard_map/all_gather | solution.py:48
  114.3 0.0 copy-start.4
  114.4 3.9 %convolution_convert_fusion.2 = bf16[96,512]{1,0:T(8,128)(2,1)S(1)} fusion(bf16[96,6144]{1,0:T(8,128)(2,1)S(1)} %bitcast.45, bf16[6144,512]{1,0:T(8,128)(2,1)} %all-gather.4.cloned.1.call-done), kind=kOutput, calls=%fused_computation.7 | convolution fusion | flops 604028928 | bytes 7569408 | tf_op jit(solution)/shard_map/dot_general | solution.py:53
  118.3 0.0 copy-start.1
  118.3 0.0 copy-done.4
  118.3 5.2 %fusion = (f32[]{:T(128)}, f32[]{:T(128)}, bf16[96,512]{1,0:T(8,128)(2,1)}) fusion(bf16[96,512]{1,0:T(8,128)(2,1)S(1)} %copy-done.4, bf16[96,512]{1,0:T(8,128)(2,1)S(1)} %convolution_convert_fusion.2, bf16[96,6144]{1,0:T(8,128)(2,1)S(1)} %bitcast.42, bf16[6144,512]{1,0:T(8,128)(2,1)} %all-gather.4.cloned.1.call-done), kind=kOutput, calls=%fused_computation.13 | convolution fusion | flops 604372992 | bytes 7766024 | tf_op jit(solution)/shard_map/dot_general | solution.py:53
  123.5 0.0 copy-done.1
  123.5 0.1 all-gather.6.cloned.1.call-update
  123.6 0.1 all-gather.8.cloned.1.call-start
  123.7 0.7 all-gather.8.cloned.1.call-update
  124.4 1.2 pad_maximum_fusion
  125.6 12.1 %psum.21 = f32[2]{0:T(128)S(1)} all-reduce(f32[2]{0:T(128)S(1)} %pad_maximum_fusion), channel_id=1, replica_groups=mesh['grp'=2,'row_0'=8,'row_1'=8,'col'=2] {'row_0'}, use_global_device_ids=true, to_apply=%region_2.0 | all-reduce | flops 2 | bytes 16 | tf_op jit(solution)/shard_map/psum | solution.py:43
  137.7 12.8 %psum.22 = f32[2]{0:T(128)S(1)} all-reduce(f32[2]{0:T(128)S(1)} %psum.21), channel_id=1, replica_groups=mesh['grp'=2,'row_0'=8,'row_1'=8,'col'=2] {'row_1'}, use_global_device_ids=true, to_apply=%region_3.0 | all-reduce | flops 2 | bytes 16 | tf_op jit(solution)/shard_map/psum | solution.py:43
  150.5 11.3 %psum.23 = f32[2]{0:T(128)S(1)} all-reduce(f32[2]{0:T(128)S(1)} %psum.22), channel_id=1, replica_groups=mesh['grp'=2,'row_0'=8,'row_1'=8,'col'=2] {'col'}, use_global_device_ids=true, to_apply=%region_4.0 | all-reduce | flops 2 | bytes 16 | tf_op jit(solution)/shard_map/psum | solution.py:43
  161.8 0.6 fusion.2
  162.4 45.8 %all-gather.6.cloned.1.call-done = bf16[6144,512]{1,0:T(8,128)(2,1)} async-done(((bf16[96,512]{1,0:T(8,128)(2,1)}), bf16[6144,512]{1,0:T(8,128)(2,1)}) %all-gather.6.cloned.1.call-update) | async-done | bytes 6291472 | tf_op jit(solution)/shard_map/all_gather | solution.py:60
  208.2 4.8 %convolution_convert_fusion.1 = bf16[96,6144]{1,0:T(8,128)(2,1)S(1)} fusion(bf16[96,512]{1,0:T(8,128)(2,1)} %get-tuple-element.11, bf16[6144,512]{1,0:T(8,128)(2,1)} %all-gather.6.cloned.1.call-done), kind=kOutput, calls=%fused_computation.1 | convolution fusion | flops 604569600 | bytes 7569408 | tf_op jit(solution)/shard_map/dot_general | solution.py:58
  213.1 1.1 copy.15
  214.2 0.0 copy-start.2
  214.2 6.1 %all-to-all-start.2 = ((bf16[2,96,3072]{2,1,0:T(8,128)(2,1)}), bf16[2,96,3072]{2,1,0:T(8,128)(2,1)S(1)}, u32[]{:S(2)}, u32[]{:S(2)}) async-start(bf16[2,96,3072]{2,1,0:T(8,128)(2,1)} %bitcast.39), calls=%async_computation.2 | async-start | bytes 2359296 | tf_op jit(solution)/shard_map/all_to_all | solution.py:38
  220.2 74.9 %all-gather.8.cloned.1.call-done = bf16[6144,512]{1,0:T(8,128)(2,1)} async-done(((bf16[96,512]{1,0:T(8,128)(2,1)}), bf16[6144,512]{1,0:T(8,128)(2,1)}) %all-gather.8.cloned.1.call-update) | async-done | bytes 6291472 | tf_op jit(solution)/shard_map/all_gather | solution.py:60
  295.2 0.0 copy-done.2
  295.2 4.8 %convolution_convert_fusion = bf16[96,6144]{1,0:T(8,128)(2,1)S(1)} fusion(bf16[96,512]{1,0:T(8,128)(2,1)S(1)} %copy-done.2, bf16[6144,512]{1,0:T(8,128)(2,1)} %all-gather.8.cloned.1.call-done), kind=kOutput, calls=%fused_computation | convolution fusion | flops 604569600 | bytes 7569408 | tf_op jit(solution)/shard_map/dot_general | solution.py:58
  300.0 1.1 copy.14
  301.1 0.0 all-to-all-done.2
  301.1 5.9 %all-to-all-start.3 = ((bf16[2,96,3072]{2,1,0:T(8,128)(2,1)}), bf16[2,96,3072]{2,1,0:T(8,128)(2,1)S(1)}, u32[]{:S(2)}, u32[]{:S(2)}) async-start(bf16[2,96,3072]{2,1,0:T(8,128)(2,1)} %bitcast.37), calls=%async_computation.3 | async-start | bytes 2359296 | tf_op jit(solution)/shard_map/all_to_all | solution.py:38
  307.0 0.2 convert_reduce_fusion.1
  307.2 0.0 copy-start
  307.2 1.6 all-to-all-done.3
  308.8 0.0 copy-start.3
  308.8 0.2 convert_reduce_fusion
  309.1 0.0 copy-done
  309.1 0.8 copy-done.3
  309.9 2.4 subtract_convert_fusion
Async XLA Ops:
  6.5 107.8 %all-gather.4.cloned.1.call-start = ((), (), s32[]{:S(2)}) async-start(), calls=%async_computation.4 | async-start | bytes 6389760 | tf_op jit(solution)/shard_map/all_gather | solution.py:48
  34.7 5.8 %all-to-all-start = ((bf16[2,96,3072]{2,1,0:T(8,128)(2,1)}), bf16[2,96,3072]{2,1,0:T(8,128)(2,1)S(1)}, u32[]{:S(2)}, u32[]{:S(2)}) async-start(bf16[2,96,3072]{2,1,0:T(8,128)(2,1)} %broadcast_in_dim.15), calls=%async_computation | async-start | bytes 2359296 | tf_op jit(solution)/shard_map/all_to_all | solution.py:15
  38.7 169.6 %all-gather.6.cloned.1.call-start = ((), (), s32[]{:S(2)}) async-start(), calls=%async_computation.5 | async-start | bytes 6389760 | tf_op jit(solution)/shard_map/all_gather | solution.py:60
  114.3 4.0 %copy-start.4 = (bf16[96,512]{1,0:T(8,128)(2,1)S(1)}, bf16[96,512]{1,0:T(8,128)(2,1)}, u32[]{:S(2)}) copy-start(bf16[96,512]{1,0:T(8,128)(2,1)} %param.4) | copy-start | bytes 294916
  118.3 5.2 %copy-start.1 = (bf16[96,512]{1,0:T(8,128)(2,1)}, bf16[96,512]{1,0:T(8,128)(2,1)S(1)}, u32[]{:S(2)}) copy-start(bf16[96,512]{1,0:T(8,128)(2,1)S(1)} %convolution_convert_fusion.2) | copy-start | bytes 294916
  123.6 171.6 %all-gather.8.cloned.1.call-start = ((), (), s32[]{:S(2)}) async-start(), calls=%async_computation.6 | async-start | bytes 6389760 | tf_op jit(solution)/shard_map/all_gather | solution.py:60
  214.2 81.0 %copy-start.2 = (bf16[96,512]{1,0:T(8,128)(2,1)S(1)}, bf16[96,512]{1,0:T(8,128)(2,1)}, u32[]{:S(2)}) copy-start(bf16[96,512]{1,0:T(8,128)(2,1)} %copy-done.1) | copy-start | bytes 294916
  214.2 86.9 %all-to-all-start.2 = ((bf16[2,96,3072]{2,1,0:T(8,128)(2,1)}), bf16[2,96,3072]{2,1,0:T(8,128)(2,1)S(1)}, u32[]{:S(2)}, u32[]{:S(2)}) async-start(bf16[2,96,3072]{2,1,0:T(8,128)(2,1)} %bitcast.39), calls=%async_computation.2 | async-start | bytes 2359296 | tf_op jit(solution)/shard_map/all_to_all | solution.py:38
  301.1 7.8 %all-to-all-start.3 = ((bf16[2,96,3072]{2,1,0:T(8,128)(2,1)}), bf16[2,96,3072]{2,1,0:T(8,128)(2,1)S(1)}, u32[]{:S(2)}, u32[]{:S(2)}) async-start(bf16[2,96,3072]{2,1,0:T(8,128)(2,1)} %bitcast.37), calls=%async_computation.3 | async-start | bytes 2359296 | tf_op jit(solution)/shard_map/all_to_all | solution.py:38
  307.2 1.8 copy-start
  308.8 1.1 copy-start.3
Sparse Core Ops, SparseCore 0:
  9.8 104.4 all-gather.3
  123.7 84.4 all-gather.5
  210.7 84.4 all-gather.7
where the time goes:
time: 320 us; the launch traced here: 319 us
  waiting for transfers between devices  199 us (62%)
  blocking collectives  60.9 us (19%)
  matrix products  18.8 us (6%)
  starting transfers between devices  16 us (5%)
  between operations  13.2 us (4%)
  local copies, waits for them, and re-layouts  6.48 us (2%)
  other arithmetic  4.08 us (1%)
    all_gather x2, waiting for transfers between devices, shards(): lax.all_gather(half_local, ROW, axis=0, tiled=True)  121 us
    all_gather x1, waiting for transfers between devices, shards(): all_orbitals = lax.all_gather(orbitals, ROW, axis=0, tiled=True)  73.8 us
    psum x3, blocking collectives, by_axis(): return functools.reduce(lax.psum, axes, value)  36.1 us
    all_to_all x1, blocking collectives, copy_for_each(): lax.all_to_all(jnp.broadcast_to(value[None], (size, *value.shape)), axis,...  24.7 us
    all_to_all x2, starting transfers between devices, sum_at_owner(): lax.all_to_all(tiles, axis, split_axis=0, concat_axis=0, tiled=True)  12 us
    dot_general x2, matrix products, shards(): lax.dot_general(half_local, lax.all_gather(half_local, ROW, axis=0, tiled...  9.64 us
    dot_general x2, matrix products, shards(): jnp.dot(collect(factors[aux], 'col', 1), all_orbitals, preferred_element_...  9.15 us
  transfers between devices with their start and end apart: 6, of which 5 were waited for; matrix products, arithmetic and copies ran while one was open for 5% of the time, Pallas kernels for 0%

commit v1 on v0

--- a/solution.py
+++ b/solution.py
@@ -45,7 +45,9 @@
 
 def shards(factors, orbitals, field_term):
     aux_count = factors.shape[0]
-    all_orbitals = lax.all_gather(orbitals, ROW, axis=0, tiled=True)
+    all_orbitals = jnp.concatenate(
+        lax.all_to_all(jnp.stack([orbitals] * lax.axis_size(ROW)), ROW, 0, 0), axis=0
+    )
     orbit_wide = orbitals.astype(jnp.float32)
     exchange = None
     gammas = []

time: 320 us -> 474 us (1.48)
  waiting for transfers between devices: 199 us -> 316 us
  blocking collectives: 60.9 us -> 92.4 us
    all_to_all x1, waiting for transfers between devices: 1.74 us -> 171 us  [shards(): lax.all_to_all(jnp.stack([orbitals] * lax.axis_size(ROW)), ROW, 0, 0)]
    all_gather x1 -> x0, waiting for transfers between devices: 73.8 us -> none  [shards(): all_orbitals = lax.all_gather(orbitals, ROW, axis=0, tiled=True)]
    psum x3, blocking collectives: 36.1 us -> 62.9 us  [by_axis(): return functools.reduce(lax.psum, axes, value)]
    all_gather x2, waiting for transfers between devices: 121 us -> 142 us  [shards(): lax.all_gather(half_local, ROW, axis=0, tiled=True)]
    all_to_all x1 -> x2, blocking collectives: 24.7 us -> 29.6 us  [copy_for_each(): lax.all_to_all(jnp.broadcast_to(value[None], (size, *value.shape)), axis,...]
  transfers between devices with their start and end apart: 6 -> 5, of which waited for: 5 -> 4; matrix products, arithmetic and copies ran while one was open for 5% -> 3% of each run, Pallas kernels for 0% -> 0%
where the time goes in v1:
time: 474 us; the launch traced here: 473 us
  waiting for transfers between devices  316 us (67%)
  blocking collectives  92.4 us (19%)
  starting transfers between devices  19.5 us (4%)
  matrix products  18.8 us (4%)
  between operations  13.6 us (3%)
  local copies, waits for them, and re-layouts  8.85 us (2%)
    all_to_all x1, waiting for transfers between devices, shards(): lax.all_to_all(jnp.stack([orbitals] * lax.axis_size(ROW)), ROW, 0, 0)  171 us
    all_gather x2, waiting for transfers between devices, shards(): lax.all_gather(half_local, ROW, axis=0, tiled=True)  142 us
    psum x3, blocking collectives, by_axis(): return functools.reduce(lax.psum, axes, value)  62.9 us
    all_to_all x2, blocking collectives, copy_for_each(): lax.all_to_all(jnp.broadcast_to(value[None], (size, *value.shape)), axis,...  29.6 us
    all_to_all x2, starting transfers between devices, sum_at_owner(): lax.all_to_all(tiles, axis, split_axis=0, concat_axis=0, tiled=True)  12 us
    dot_general x2, matrix products, shards(): lax.dot_general(half_local, lax.all_gather(half_local, ROW, axis=0, tiled...  9.64 us
  transfers between devices with their start and end apart: 5, of which 4 were waited for; matrix products, arithmetic and copies ran while one was open for 3% of the time, Pallas kernels for 0%

profile of v1, /device:TPU:513, one launch (start us, length us, event | category | flops | bytes accessed | tf_op | source)
XLA Modules:
  0.0 473.1 jit_solution(11344253183871000055)
XLA Ops:
  6.5 1.3 slice_bitcast_fusion
  7.9 0.1 broadcast_in_dim.17
  8.0 24.7 %all_to_all.25 = bf16[2,96,3072]{2,1,0:T(8,128)(2,1)S(1)} all-to-all(bf16[2,96,3072]{2,1,0:T(8,128)(2,1)S(1)} %broadcast_in_dim.17), channel_id=1, replica_groups=mesh['grp'=2,'row_0'=8,'row_1'=8,'col'=2] {'col'}, dimensions={0} | all-to-all | bytes 2359296 | tf_op jit(solution)/shard_map/all_to_all | solution.py:15
  32.7 0.1 broadcast_in_dim.15
  32.9 0.0 copy-start.4
  32.9 4.8 %all_to_all.26 = bf16[2,96,3072]{2,1,0:T(8,128)(2,1)S(1)} all-to-all(bf16[2,96,3072]{2,1,0:T(8,128)(2,1)S(1)} %broadcast_in_dim.15), channel_id=1, replica_groups=mesh['grp'=2,'row_0'=8,'row_1'=8,'col'=2] {'col'}, dimensions={0} | all-to-all | bytes 2359296 | tf_op jit(solution)/shard_map/all_to_all | solution.py:15
  37.7 0.0 copy-done.4
  37.7 3.4 stack.8
  41.1 7.4 %all-to-all-start.1 = ((bf16[64,96,512]{2,1,0:T(8,128)(2,1)}), bf16[64,96,512]{2,1,0:T(8,128)(2,1)}, u32[]{:S(2)}, u32[]{:S(2)}) async-start(bf16[64,96,512]{2,1,0:T(8,128)(2,1)} %stack.8), calls=%async_computation.1 | async-start | bytes 12582912 | tf_op jit(solution)/shard_map/all_to_all | solution.py:49
  48.5 0.1 all-gather.3.cloned.1.call-start
  48.6 0.1 copy.11
  48.7 0.1 copy.10
  48.8 170.7 %all-to-all-done.1 = bf16[64,96,512]{2,1,0:T(8,128)(2,1)} async-done(((bf16[64,96,512]{2,1,0:T(8,128)(2,1)}), bf16[64,96,512]{2,1,0:T(8,128)(2,1)}, u32[]{:S(2)}, u32[]{:S(2)}) %all-to-all-start.1) | async-done | bytes 6291488 | tf_op jit(solution)/shard_map/all_to_all | solution.py:49
  219.5 0.0 copy-start.5
  219.5 3.9 convolution_convert_fusion.2
  223.5 0.0 copy-start.1
  223.5 0.0 copy-done.5
  223.5 5.3 %fusion = (f32[]{:T(128)}, f32[]{:T(128)}, bf16[96,512]{1,0:T(8,128)(2,1)}) fusion(bf16[96,512]{1,0:T(8,128)(2,1)S(1)} %copy-done.5, bf16[96,512]{1,0:T(8,128)(2,1)S(1)} %convolution_convert_fusion.2, bf16[96,6144]{1,0:T(8,128)(2,1)S(1)} %bitcast.43, bf16[6144,512]{1,0:T(8,128)(2,1)} %bitcast.2), kind=kOutput, calls=%fused_computation.13 | convolution fusion | flops 604372992 | bytes 7766024 | tf_op jit(solution)/shard_map/dot_general | solution.py:55
  228.7 0.0 copy-done.1
  228.7 0.1 all-gather.3.cloned.1.call-update
  228.8 0.1 all-gather.5.cloned.1.call-start
  228.9 0.7 all-gather.5.cloned.1.call-update
  229.6 1.4 pad_maximum_fusion
  231.0 36.2 %psum.21 = f32[2]{0:T(128)S(1)} all-reduce(f32[2]{0:T(128)S(1)} %pad_maximum_fusion), channel_id=1, replica_groups=mesh['grp'=2,'row_0'=8,'row_1'=8,'col'=2] {'row_0'}, use_global_device_ids=true, to_apply=%region_2.0 | all-reduce | flops 2 | bytes 16 | tf_op jit(solution)/shard_map/psum | solution.py:43
  267.3 16.8 %psum.22 = f32[2]{0:T(128)S(1)} all-reduce(f32[2]{0:T(128)S(1)} %psum.21), channel_id=1, replica_groups=mesh['grp'=2,'row_0'=8,'row_1'=8,'col'=2] {'row_1'}, use_global_device_ids=true, to_apply=%region_3.0 | all-reduce | flops 2 | bytes 16 | tf_op jit(solution)/shard_map/psum | solution.py:43
  284.0 9.9 %psum.23 = f32[2]{0:T(128)S(1)} all-reduce(f32[2]{0:T(128)S(1)} %psum.22), channel_id=1, replica_groups=mesh['grp'=2,'row_0'=8,'row_1'=8,'col'=2] {'col'}, use_global_device_ids=true, to_apply=%region_4.0 | all-reduce | flops 2 | bytes 16 | tf_op jit(solution)/shard_map/psum | solution.py:43
  293.9 0.6 fusion.2
  294.5 67.5 %all-gather.3.cloned.1.call-done = bf16[6144,512]{1,0:T(8,128)(2,1)} async-done(((bf16[96,512]{1,0:T(8,128)(2,1)}), bf16[6144,512]{1,0:T(8,128)(2,1)}) %all-gather.3.cloned.1.call-update) | async-done | bytes 6291472 | tf_op jit(solution)/shard_map/all_gather | solution.py:62
  362.0 4.9 %convolution_convert_fusion.1 = bf16[96,6144]{1,0:T(8,128)(2,1)S(1)} fusion(bf16[96,512]{1,0:T(8,128)(2,1)} %get-tuple-element.11, bf16[6144,512]{1,0:T(8,128)(2,1)} %all-gather.3.cloned.1.call-done), kind=kOutput, calls=%fused_computation.1 | convolution fusion | flops 604569600 | bytes 7569408 | tf_op jit(solution)/shard_map/dot_general | solution.py:60
  366.8 1.1 copy.15
  367.9 0.0 copy-start.2
  367.9 6.1 %all-to-all-start.3 = ((bf16[2,96,3072]{2,1,0:T(8,128)(2,1)}), bf16[2,96,3072]{2,1,0:T(8,128)(2,1)S(1)}, u32[]{:S(2)}, u32[]{:S(2)}) async-start(bf16[2,96,3072]{2,1,0:T(8,128)(2,1)} %bitcast.40), calls=%async_computation.3 | async-start | bytes 2359296 | tf_op jit(solution)/shard_map/all_to_all | solution.py:38
  374.0 74.9 %all-gather.5.cloned.1.call-done = bf16[6144,512]{1,0:T(8,128)(2,1)} async-done(((bf16[96,512]{1,0:T(8,128)(2,1)}), bf16[6144,512]{1,0:T(8,128)(2,1)}) %all-gather.5.cloned.1.call-update) | async-done | bytes 6291472 | tf_op jit(solution)/shard_map/all_gather | solution.py:62
  448.9 0.0 copy-done.2
  448.9 4.8 %convolution_convert_fusion = bf16[96,6144]{1,0:T(8,128)(2,1)S(1)} fusion(bf16[96,512]{1,0:T(8,128)(2,1)S(1)} %copy-done.2, bf16[6144,512]{1,0:T(8,128)(2,1)} %all-gather.5.cloned.1.call-done), kind=kOutput, calls=%fused_computation | convolution fusion | flops 604569600 | bytes 7569408 | tf_op jit(solution)/shard_map/dot_general | solution.py:60
  453.7 1.1 copy.14
  454.8 0.0 all-to-all-done.3
  454.8 5.9 %all-to-all-start.4 = ((bf16[2,96,3072]{2,1,0:T(8,128)(2,1)}), bf16[2,96,3072]{2,1,0:T(8,128)(2,1)S(1)}, u32[]{:S(2)}, u32[]{:S(2)}) async-start(bf16[2,96,3072]{2,1,0:T(8,128)(2,1)} %bitcast.38), calls=%async_computation.4 | async-start | bytes 2359296 | tf_op jit(solution)/shard_map/all_to_all | solution.py:38
  460.7 0.2 convert_reduce_fusion.1
  460.9 0.0 copy-start
  461.0 1.6 all-to-all-done.4
  462.6 0.0 copy-start.3
  462.6 0.2 convert_reduce_fusion
  462.8 0.0 copy-done
  462.8 0.8 copy-done.3
  463.6 2.6 subtract_convert_fusion
Async XLA Ops:
  32.9 4.8 %copy-start.4 = (bf16[96,512]{1,0:T(8,128)(2,1)S(1)}, bf16[96,512]{1,0:T(8,128)(2,1)}, u32[]{:S(2)}) copy-start(bf16[96,512]{1,0:T(8,128)(2,1)} %param.4) | copy-start | bytes 294916
  41.1 178.4 %all-to-all-start.1 = ((bf16[64,96,512]{2,1,0:T(8,128)(2,1)}), bf16[64,96,512]{2,1,0:T(8,128)(2,1)}, u32[]{:S(2)}, u32[]{:S(2)}) async-start(bf16[64,96,512]{2,1,0:T(8,128)(2,1)} %stack.8), calls=%async_computation.1 | async-start | bytes 12582912 | tf_op jit(solution)/shard_map/all_to_all | solution.py:49
  48.5 313.5 %all-gather.3.cloned.1.call-start = ((), (), s32[]{:S(2)}) async-start(), calls=%async_computation.5 | async-start | bytes 6389760 | tf_op jit(solution)/shard_map/all_gather | solution.py:62
  219.5 4.0 copy-start.5
  223.5 5.3 %copy-start.1 = (bf16[96,512]{1,0:T(8,128)(2,1)}, bf16[96,512]{1,0:T(8,128)(2,1)S(1)}, u32[]{:S(2)}) copy-start(bf16[96,512]{1,0:T(8,128)(2,1)S(1)} %convolution_convert_fusion.2) | copy-start | bytes 294916
  228.8 220.1 %all-gather.5.cloned.1.call-start = ((), (), s32[]{:S(2)}) async-start(), calls=%async_computation.6 | async-start | bytes 6389760 | tf_op jit(solution)/shard_map/all_gather | solution.py:62
  367.9 81.0 %copy-start.2 = (bf16[96,512]{1,0:T(8,128)(2,1)S(1)}, bf16[96,512]{1,0:T(8,128)(2,1)}, u32[]{:S(2)}) copy-start(bf16[96,512]{1,0:T(8,128)(2,1)} %copy-done.1) | copy-start | bytes 294916
  367.9 86.9 %all-to-all-start.3 = ((bf16[2,96,3072]{2,1,0:T(8,128)(2,1)}), bf16[2,96,3072]{2,1,0:T(8,128)(2,1)S(1)}, u32[]{:S(2)}, u32[]{:S(2)}) async-start(bf16[2,96,3072]{2,1,0:T(8,128)(2,1)} %bitcast.40), calls=%async_computation.3 | async-start | bytes 2359296 | tf_op jit(solution)/shard_map/all_to_all | solution.py:38
  454.8 7.8 %all-to-all-start.4 = ((bf16[2,96,3072]{2,1,0:T(8,128)(2,1)}), bf16[2,96,3072]{2,1,0:T(8,128)(2,1)S(1)}, u32[]{:S(2)}, u32[]{:S(2)}) async-start(bf16[2,96,3072]{2,1,0:T(8,128)(2,1)} %bitcast.38), calls=%async_computation.4 | async-start | bytes 2359296 | tf_op jit(solution)/shard_map/all_to_all | solution.py:38
  460.9 1.8 copy-start
  462.6 1.1 copy-start.3
Sparse Core Ops, SparseCore 0:
  228.9 132.9 all-gather.2
  364.4 84.4 all-gather.4
